TPU v7x, 32 devices: a whole 2x2x4 slice. The times are simulated.
32 devices in a mesh: member: 8 (over y, x, core), strip: 4 (over z).
Axes of the slice: x: 2, y: 2, z: 4, core: 2. Of those that a mesh axis runs over, the one named last changes fastest.
Arguments:
- sample_fields: float32 [64, 3, 64, 1024], P('member', None, 'strip'), may hold values from -0.8 to 0.8
- report_counts: int32 [4, 8], P('strip', 'member'), may hold values from 1 to 256, as said below
- report_cells: int32 [4, 8, 256], P('strip', 'member'), may hold values from 0 to 2047
- report_values: float32 [4, 8, 256], P('strip', 'member'), may hold values from -1.5 to 1.5
- report_errors: float32 [4, 8, 256], P('strip', 'member'), may hold values from 0.04 to 0.2
- local_radius: int32 [4, 8], P('strip', 'member'), may hold values from 1 to 3
Outputs:
- analysis: float32 [64, 3, 64, 1024], P('member', None, 'strip')
Inputs may be any that keep to these rules, and one draw needn't show every extreme that they name: `report_counts`: counts lie between 1 and 256; 256 is reached by some region in every draw; slots from the count on are not used.
All inputs are finite; a program needn't handle non-finite values.
Results may differ from a plain program's by a relative error of at most 0.0003.
Values sent between devices are 32-bit elements; how exact they have to be, the bound alone decides.
No kernel may reach another device: no remote copies, remote signals or barrier semaphores. Data moves between devices by JAX's collectives and lax.ppermute only.
A program may use at most 64 MiB of HBM per device.

v0:
```python
import jax
import jax.numpy as jnp
from jax import lax
from jax.sharding import PartitionSpec as P

BAND_HEIGHT_CELLS = 16
PATCH_WIDTH_CELLS = 128
STEPS = 12
TURNS = 20
COURANT = 0.125
GRAVITY = 1.0
ROTATION = 0.05
HIGHEST_PRECISION = lax.Precision.HIGHEST


def with_halo(block, sides, width):
    for axis, dim in sides:
        count = lax.axis_size(axis)
        forward = [(i, i + 1) for i in range(count - 1)]
        forward.append((count - 1, 0))
        backward = [(target, source) for source, target in forward]
        low = lax.ppermute(
            lax.slice_in_dim(block, block.shape[dim] - width, None, axis=dim), axis, forward
        )
        high = lax.ppermute(lax.slice_in_dim(block, 0, width, axis=dim), axis, backward)
        block = jnp.concatenate([low, block, high], axis=dim)
    return block


def to_east(field):
    return field[..., 1:-1, 2:]


def to_west(field):
    return field[..., 1:-1, :-2]


def to_north(field):
    return field[..., 2:, 1:-1]


def to_south(field):
    return field[..., :-2, 1:-1]


def middle(field):
    return field[..., 1:-1, 1:-1]


def neighbour_mean(field):
    return 0.25 * (to_east(field) + to_west(field) + to_north(field) + to_south(field))


def advance_once(padded):
    height = padded[:, 0]
    flow_x = padded[:, 1]
    flow_y = padded[:, 2]
    column_depth = 1.0 + height
    flux_x = column_depth * flow_x
    flux_y = column_depth * flow_y
    centre_x = middle(flow_x)
    centre_y = middle(flow_y)
    new_height = neighbour_mean(height) - COURANT * (
        to_east(flux_x) - to_west(flux_x) + to_north(flux_y) - to_south(flux_y)
    )
    new_flow_x = (
        neighbour_mean(flow_x)
        - COURANT
        * (
            centre_x * (to_east(flow_x) - to_west(flow_x))
            + centre_y * (to_north(flow_x) - to_south(flow_x))
            + GRAVITY * (to_east(height) - to_west(height))
        )
        + ROTATION * centre_y
    )
    new_flow_y = (
        neighbour_mean(flow_y)
        - COURANT
        * (
            centre_x * (to_east(flow_y) - to_west(flow_y))
            + centre_y * (to_north(flow_y) - to_south(flow_y))
            + GRAVITY * (to_north(height) - to_south(height))
        )
        - ROTATION * centre_x
    )
    return jnp.stack([new_height, new_flow_x, new_flow_y], axis=1)


def observe(region, locations, values, errors, live_count):
    observed = jnp.take(region, locations, axis=1)
    observed_mean = jnp.mean(observed, axis=0)
    spread = observed - observed_mean[None, :]
    innovation = values - observed_mean
    slot_ids = jnp.arange(locations.shape[0])
    precision = jnp.where(slot_ids < live_count, 1.0 / errors, 0.0 * errors)
    row_pos = ((locations // PATCH_WIDTH_CELLS).astype(jnp.float32) + 0.5) / BAND_HEIGHT_CELLS - 0.5
    col_pos = ((locations % PATCH_WIDTH_CELLS).astype(jnp.float32) + 0.5) / PATCH_WIDTH_CELLS - 0.5
    return jnp.concatenate(
        [spread, innovation[None], precision[None], row_pos[None], col_pos[None]], axis=0
    )


def analyse(region, neighbours, radius_blocks):
    sample_collection = region.shape[0]
    offsets = jnp.arange(3).astype(region.dtype) - 1.0
    anomalies = neighbours[:, :, :sample_collection, :]
    innovation = neighbours[:, :, sample_collection, :].reshape(-1)
    precision = neighbours[:, :, sample_collection + 1, :]
    row_pos = neighbours[:, :, sample_collection + 2, :] + offsets[:, None, None]
    col_pos = neighbours[:, :, sample_collection + 3, :] + offsets[None, :, None]
    radius_float = radius_blocks.astype(region.dtype)
    tapering = jnp.exp(
        -0.5 * (row_pos * row_pos + col_pos * col_pos) / (radius_float * radius_float)
    )
    weights = (tapering * precision).reshape(-1)
    spread = jnp.transpose(anomalies, (2, 0, 1, 3)).reshape(sample_collection, -1)
    weighted = spread * weights[None, :]
    ensemble_scale = sample_collection - 1.0
    identity = jnp.eye(sample_collection, dtype=region.dtype)
    gram_matrix = jnp.dot(weighted, spread.T, precision=HIGHEST_PRECISION)
    normal = identity + gram_matrix / ensemble_scale
    pull_vector = jnp.dot(weighted, innovation, precision=HIGHEST_PRECISION)
    frob_norm = jnp.sqrt(jnp.sum(normal * normal))
    iterate = normal / frob_norm
    inverse_root = identity
    for newton_turn in range(TURNS):
        factor = 1.5 * identity - 0.5 * jnp.dot(inverse_root, iterate, precision=HIGHEST_PRECISION)
        iterate = jnp.dot(iterate, factor, precision=HIGHEST_PRECISION)
        inverse_root = jnp.dot(factor, inverse_root, precision=HIGHEST_PRECISION)
    root_inverse = inverse_root / jnp.sqrt(frob_norm)
    full_inverse = jnp.dot(inverse_root, inverse_root, precision=HIGHEST_PRECISION) / frob_norm
    mean_weights = jnp.dot(full_inverse, pull_vector, precision=HIGHEST_PRECISION) / ensemble_scale
    transform = root_inverse + mean_weights[:, None]
    centre = jnp.mean(region, axis=0)
    deviations = region - centre[None, :]
    return centre[None, :] + jnp.dot(transform.T, deviations, precision=HIGHEST_PRECISION)


def strip_block(current_state, halo_depth):
    padded = with_halo(current_state, (("strip", 2),), halo_depth)
    padded = jnp.concatenate([padded[..., -halo_depth:], padded, padded[..., :halo_depth]], axis=3)
    for repeat in range(halo_depth):
        padded = advance_once(padded)
    return padded


def on_device(
    sample_fields, report_counts, report_cells, report_values, report_errors, local_radius
):
    own_members, fields, row_count, grid_cols = sample_fields.shape
    blocks = lax.axis_size("member")
    region_cols = grid_cols // blocks
    sample_collection = own_members * blocks
    halo_depth = 3
    rounds = STEPS // halo_depth

    def strip_round(counter, carried):
        return strip_block(carried, halo_depth)

    current_state = lax.fori_loop(0, rounds, strip_round, sample_fields)
    by_block = current_state.reshape(own_members, fields, row_count, blocks, region_cols)
    current_state = lax.all_to_all(by_block, "member", split_axis=3, concat_axis=0, tiled=True)
    region = current_state.reshape(sample_collection, fields * row_count * region_cols)
    packed = observe(
        region, report_cells[0, 0], report_values[0, 0], report_errors[0, 0], report_counts[0, 0]
    )
    neighbours = with_halo(packed[None, None], (("member", 1), ("strip", 0)), 1)
    updated = analyse(region, neighbours, local_radius[0, 0])
    outgoing = updated.reshape(sample_collection, fields, row_count, 1, region_cols)
    returned = lax.all_to_all(outgoing, "member", split_axis=0, concat_axis=3, tiled=True)
    return returned.reshape(own_members, fields, row_count, grid_cols)


def solution(mesh):
    in_specs = (
        P("member", None, "strip", None),
        P("strip", "member"),
        P("strip", "member", None),
        P("strip", "member", None),
        P("strip", "member", None),
        P("strip", "member"),
    )
    out_specs = P("member", None, "strip", None)
    return jax.shard_map(
        on_device, mesh=mesh, in_specs=in_specs, out_specs=out_specs, check_vma=False
    )
```

profile of v0, /device:TPU:0, one launch (start us, length us, event | category | flops | bytes accessed | tf_op | source)
XLA Modules:
  0.0 245.0 jit_solution(7391086606007713092)
XLA Ops:
  1.5 151.1 %while.10 = (s32[]{:T(128)}, f32[8,3,16,1024]{3,2,0,1:T(8,128)S(1)}, s32[]{:T(128)}) while((s32[]{:T(128)}, f32[8,3,16,1024]{3,2,0,1:T(8,128)S(1)}, s32[]{:T(128)}) %tuple.56), condition=%wide.region_1.0_spmd, body=%wide.region_0.0_spmd.sunk | while | flops 20949056 | bytes 80089624 | solution.py:160
  1.7 5.1 %collective-permute-start = (f32[8,3,3,1024]{3,2,0,1:T(4,128)S(1)}, f32[8,3,3,1024]{3,2,0,1:T(4,128)S(1)}, u32[]{:S(2)}, u32[]{:S(2)}) collective-permute-start(f32[8,3,3,1024]{3,2,0,1:T(4,128)S(1)} %get-tuple-element.91), channel_id=1, source_target_pairs={{1,0},{2,1},{3,2},{0,3},{5,4},{6,5},{7,6},{4,7},{9,8},{10,9},{11,1... | collective-permute-start | bytes 884744 | tf_op jit(solution)/shard_map/while/body/eval_jaxpr/ppermute | solution.py:25
  6.8 9.5 %collective-permute-done = f32[8,3,3,1024]{3,2,0,1:T(4,128)S(1)} collective-permute-done((f32[8,3,3,1024]{3,2,0,1:T(4,128)S(1)}, f32[8,3,3,1024]{3,2,0,1:T(4,128)S(1)}, u32[]{:S(2)}, u32[]{:S(2)}) %collective-permute-start) | collective-permute-done | bytes 294944 | tf_op jit(solution)/shard_map/while/body/eval_jaxpr/ppermute | solution.py:25
  16.3 8.2 %collective-permute-done.1 = f32[8,3,3,1024]{3,2,0,1:T(4,128)S(1)} collective-permute-done((f32[8,3,3,1024]{3,2,0,1:T(4,128)S(1)}, f32[8,3,3,1024]{3,2,0,1:T(4,128)S(1)}, u32[]{:S(2)}, u32[]{:S(2)}) %collective-permute-start.1) | collective-permute-done | bytes 294944 | tf_op jit(solution)/shard_map/while/body/eval_jaxpr/ppermute | solution.py:22
  26.4 3.2 %concatenate.19 = f32[8,3,22,1030]{3,2,0,1:T(8,128)S(1)} concatenate(f32[8,3,22,3]{3,2,0,1:T(8,128)S(1)} %get-tuple-element.93, f32[8,3,22,1024]{3,2,0,1:T(8,128)} %copy-done, f32[8,3,22,3]{3,2,0,1:T(8,128)S(1)} %get-tuple-element.94), dimensions={3} | concatenate | bytes 4350720 | tf_op jit(solution)/shard_map/while/body/eval_jaxpr/concatenate | solution.py:141
  29.9 2.8 %add_multiply_fusion.12 = (f32[8,20,1028]{2,1,0:T(8,128)S(1)}, f32[8,20,1028]{2,1,0:T(8,128)S(1)}, f32[8,20,1028]{2,1,0:T(8,128)S(1)}) fusion(f32[8,22,1030]{2,1,0:T(8,128)S(1)} %get-tuple-element.95, f32[8,22,1030]{2,1,0:T(8,128)S(1)} %get-tuple-element.96, f32[8,22,1030]{2,1,0:T(8,128)S(1)} %get-tuple-element.97, ...), kind=kLoop, calls=%fused_computation.23.clone.1 | loop fusion | flops 4276480 | bytes 11184640 | tf_op jit(solution)/shard_map/while/body/eval_jaxpr/mul | solution.py:59
  34.4 2.8 %add_multiply_fusion.14 = (f32[8,18,1026]{2,1,0:T(8,128)S(1)}, f32[8,18,1026]{2,1,0:T(8,128)S(1)}, f32[8,18,1026]{2,1,0:T(8,128)S(1)}) fusion(f32[8,20,1028]{2,1,0:T(8,128)S(1)} %get-tuple-element.101, f32[8,20,1028]{2,1,0:T(8,128)S(1)} %get-tuple-element.102, f32[8,20,1028]{2,1,0:T(8,128)S(1)} %get-tuple-element.100, ...), kind=kLoop, calls=%fused_computation.21.clone.1 | loop fusion | flops 3841344 | bytes 10046592 | tf_op jit(solution)/shard_map/while/body/eval_jaxpr/mul | solution.py:59
  43.8 16.4 %collective-permute-done = f32[8,3,3,1024]{3,2,0,1:T(4,128)S(1)} collective-permute-done((f32[8,3,3,1024]{3,2,0,1:T(4,128)S(1)}, f32[8,3,3,1024]{3,2,0,1:T(4,128)S(1)}, u32[]{:S(2)}, u32[]{:S(2)}) %collective-permute-start) | collective-permute-done | bytes 294944 | tf_op jit(solution)/shard_map/while/body/eval_jaxpr/ppermute | solution.py:25
  62.1 3.2 %concatenate.19 = f32[8,3,22,1030]{3,2,0,1:T(8,128)S(1)} concatenate(f32[8,3,22,3]{3,2,0,1:T(8,128)S(1)} %get-tuple-element.93, f32[8,3,22,1024]{3,2,0,1:T(8,128)} %copy-done, f32[8,3,22,3]{3,2,0,1:T(8,128)S(1)} %get-tuple-element.94), dimensions={3} | concatenate | bytes 4350720 | tf_op jit(solution)/shard_map/while/body/eval_jaxpr/concatenate | solution.py:141
  65.7 2.8 %add_multiply_fusion.12 = (f32[8,20,1028]{2,1,0:T(8,128)S(1)}, f32[8,20,1028]{2,1,0:T(8,128)S(1)}, f32[8,20,1028]{2,1,0:T(8,128)S(1)}) fusion(f32[8,22,1030]{2,1,0:T(8,128)S(1)} %get-tuple-element.95, f32[8,22,1030]{2,1,0:T(8,128)S(1)} %get-tuple-element.96, f32[8,22,1030]{2,1,0:T(8,128)S(1)} %get-tuple-element.97, ...), kind=kLoop, calls=%fused_computation.23.clone.1 | loop fusion | flops 4276480 | bytes 11184640 | tf_op jit(solution)/shard_map/while/body/eval_jaxpr/mul | solution.py:59
  70.1 2.8 %add_multiply_fusion.14 = (f32[8,18,1026]{2,1,0:T(8,128)S(1)}, f32[8,18,1026]{2,1,0:T(8,128)S(1)}, f32[8,18,1026]{2,1,0:T(8,128)S(1)}) fusion(f32[8,20,1028]{2,1,0:T(8,128)S(1)} %get-tuple-element.101, f32[8,20,1028]{2,1,0:T(8,128)S(1)} %get-tuple-element.102, f32[8,20,1028]{2,1,0:T(8,128)S(1)} %get-tuple-element.100, ...), kind=kLoop, calls=%fused_computation.21.clone.1 | loop fusion | flops 3841344 | bytes 10046592 | tf_op jit(solution)/shard_map/while/body/eval_jaxpr/mul | solution.py:59
  77.5 2.6 %collective-permute-start = (f32[8,3,3,1024]{3,2,0,1:T(4,128)S(1)}, f32[8,3,3,1024]{3,2,0,1:T(4,128)S(1)}, u32[]{:S(2)}, u32[]{:S(2)}) collective-permute-start(f32[8,3,3,1024]{3,2,0,1:T(4,128)S(1)} %get-tuple-element.91), channel_id=1, source_target_pairs={{1,0},{2,1},{3,2},{0,3},{5,4},{6,5},{7,6},{4,7},{9,8},{10,9},{11,1... | collective-permute-start | bytes 884744 | tf_op jit(solution)/shard_map/while/body/eval_jaxpr/ppermute | solution.py:25
  80.1 9.5 %collective-permute-done = f32[8,3,3,1024]{3,2,0,1:T(4,128)S(1)} collective-permute-done((f32[8,3,3,1024]{3,2,0,1:T(4,128)S(1)}, f32[8,3,3,1024]{3,2,0,1:T(4,128)S(1)}, u32[]{:S(2)}, u32[]{:S(2)}) %collective-permute-start) | collective-permute-done | bytes 294944 | tf_op jit(solution)/shard_map/while/body/eval_jaxpr/ppermute | solution.py:25
  89.6 9.2 %collective-permute-done.1 = f32[8,3,3,1024]{3,2,0,1:T(4,128)S(1)} collective-permute-done((f32[8,3,3,1024]{3,2,0,1:T(4,128)S(1)}, f32[8,3,3,1024]{3,2,0,1:T(4,128)S(1)}, u32[]{:S(2)}, u32[]{:S(2)}) %collective-permute-start.1) | collective-permute-done | bytes 294944 | tf_op jit(solution)/shard_map/while/body/eval_jaxpr/ppermute | solution.py:22
  100.6 3.2 %concatenate.19 = f32[8,3,22,1030]{3,2,0,1:T(8,128)S(1)} concatenate(f32[8,3,22,3]{3,2,0,1:T(8,128)S(1)} %get-tuple-element.93, f32[8,3,22,1024]{3,2,0,1:T(8,128)} %copy-done, f32[8,3,22,3]{3,2,0,1:T(8,128)S(1)} %get-tuple-element.94), dimensions={3} | concatenate | bytes 4350720 | tf_op jit(solution)/shard_map/while/body/eval_jaxpr/concatenate | solution.py:141
  104.2 2.8 %add_multiply_fusion.12 = (f32[8,20,1028]{2,1,0:T(8,128)S(1)}, f32[8,20,1028]{2,1,0:T(8,128)S(1)}, f32[8,20,1028]{2,1,0:T(8,128)S(1)}) fusion(f32[8,22,1030]{2,1,0:T(8,128)S(1)} %get-tuple-element.95, f32[8,22,1030]{2,1,0:T(8,128)S(1)} %get-tuple-element.96, f32[8,22,1030]{2,1,0:T(8,128)S(1)} %get-tuple-element.97, ...), kind=kLoop, calls=%fused_computation.23.clone.1 | loop fusion | flops 4276480 | bytes 11184640 | tf_op jit(solution)/shard_map/while/body/eval_jaxpr/mul | solution.py:59
  108.7 2.8 %add_multiply_fusion.14 = (f32[8,18,1026]{2,1,0:T(8,128)S(1)}, f32[8,18,1026]{2,1,0:T(8,128)S(1)}, f32[8,18,1026]{2,1,0:T(8,128)S(1)}) fusion(f32[8,20,1028]{2,1,0:T(8,128)S(1)} %get-tuple-element.101, f32[8,20,1028]{2,1,0:T(8,128)S(1)} %get-tuple-element.102, f32[8,20,1028]{2,1,0:T(8,128)S(1)} %get-tuple-element.100, ...), kind=kLoop, calls=%fused_computation.21.clone.1 | loop fusion | flops 3841344 | bytes 10046592 | tf_op jit(solution)/shard_map/while/body/eval_jaxpr/mul | solution.py:59
  118.1 9.2 %collective-permute-done = f32[8,3,3,1024]{3,2,0,1:T(4,128)S(1)} collective-permute-done((f32[8,3,3,1024]{3,2,0,1:T(4,128)S(1)}, f32[8,3,3,1024]{3,2,0,1:T(4,128)S(1)}, u32[]{:S(2)}, u32[]{:S(2)}) %collective-permute-start) | collective-permute-done | bytes 294944 | tf_op jit(solution)/shard_map/while/body/eval_jaxpr/ppermute | solution.py:25
  127.3 8.1 %collective-permute-done.1 = f32[8,3,3,1024]{3,2,0,1:T(4,128)S(1)} collective-permute-done((f32[8,3,3,1024]{3,2,0,1:T(4,128)S(1)}, f32[8,3,3,1024]{3,2,0,1:T(4,128)S(1)}, u32[]{:S(2)}, u32[]{:S(2)}) %collective-permute-start.1) | collective-permute-done | bytes 294944 | tf_op jit(solution)/shard_map/while/body/eval_jaxpr/ppermute | solution.py:22
  137.2 3.2 %concatenate.19 = f32[8,3,22,1030]{3,2,0,1:T(8,128)S(1)} concatenate(f32[8,3,22,3]{3,2,0,1:T(8,128)S(1)} %get-tuple-element.93, f32[8,3,22,1024]{3,2,0,1:T(8,128)} %copy-done, f32[8,3,22,3]{3,2,0,1:T(8,128)S(1)} %get-tuple-element.94), dimensions={3} | concatenate | bytes 4350720 | tf_op jit(solution)/shard_map/while/body/eval_jaxpr/concatenate | solution.py:141
  140.8 2.8 %add_multiply_fusion.12 = (f32[8,20,1028]{2,1,0:T(8,128)S(1)}, f32[8,20,1028]{2,1,0:T(8,128)S(1)}, f32[8,20,1028]{2,1,0:T(8,128)S(1)}) fusion(f32[8,22,1030]{2,1,0:T(8,128)S(1)} %get-tuple-element.95, f32[8,22,1030]{2,1,0:T(8,128)S(1)} %get-tuple-element.96, f32[8,22,1030]{2,1,0:T(8,128)S(1)} %get-tuple-element.97, ...), kind=kLoop, calls=%fused_computation.23.clone.1 | loop fusion | flops 4276480 | bytes 11184640 | tf_op jit(solution)/shard_map/while/body/eval_jaxpr/mul | solution.py:59
  145.3 2.8 %add_multiply_fusion.14 = (f32[8,18,1026]{2,1,0:T(8,128)S(1)}, f32[8,18,1026]{2,1,0:T(8,128)S(1)}, f32[8,18,1026]{2,1,0:T(8,128)S(1)}) fusion(f32[8,20,1028]{2,1,0:T(8,128)S(1)} %get-tuple-element.101, f32[8,20,1028]{2,1,0:T(8,128)S(1)} %get-tuple-element.102, f32[8,20,1028]{2,1,0:T(8,128)S(1)} %get-tuple-element.100, ...), kind=kLoop, calls=%fused_computation.21.clone.1 | loop fusion | flops 3841344 | bytes 10046592 | tf_op jit(solution)/shard_map/while/body/eval_jaxpr/mul | solution.py:59
  153.0 2.1 copy.23
  155.0 3.9 %all-to-all-start = ((f32[8,3,16,8,128]{4,0,2,1,3:T(8,128)}), f32[8,3,16,8,128]{4,0,2,1,3:T(8,128)S(1)}, u32[]{:S(2)}, u32[]{:S(2)}) async-start(f32[8,3,16,8,128]{4,0,2,1,3:T(8,128)} %copy.23), calls=%async_computation | async-start | bytes 3145728 | tf_op jit(solution)/shard_map/all_to_all | solution.py:162
  160.3 19.6 %all-to-all-done = f32[8,3,16,8,128]{4,0,2,1,3:T(8,128)S(1)} async-done(((f32[8,3,16,8,128]{4,0,2,1,3:T(8,128)}), f32[8,3,16,8,128]{4,0,2,1,3:T(8,128)S(1)}, u32[]{:S(2)}, u32[]{:S(2)}) %all-to-all-start) | async-done | bytes 1572896 | tf_op jit(solution)/shard_map/all_to_all | solution.py:162
  179.9 2.3 copy.24
  182.1 2.6 %gather_fusion = f32[256,64]{1,0:T(8,128)S(1)} fusion(f32[64,6144]{0,1:T(8,128)} %copy.24, s32[1024]{0:T(1024)S(1)} %pad_clamp_fusion), kind=kCustom, calls=%fused_computation | custom fusion | bytes 132096 | tf_op jit(solution)/shard_map/jit(_take)/gather | solution.py:90
  185.0 2.6 %collective-permute-start.3 = (f32[1,1,68,256]{3,2,1,0:T(8,128)S(1)}, f32[1,1,68,256]{3,2,1,0:T(8,128)S(1)}, u32[]{:S(2)}, u32[]{:S(2)}) collective-permute-start(f32[1,1,68,256]{3,2,1,0:T(8,128)S(1)} %bitcast.266), channel_id=1, source_target_pairs={{4,0},{8,4},{12,8},{16,12},{20,16},{24,20},{28,24},{0,28},{5,1},{9... | collective-permute-start | bytes 208904 | tf_op jit(solution)/shard_map/ppermute | solution.py:25
  187.7 2.7 %collective-permute-done.2 = f32[1,1,68,256]{3,2,1,0:T(8,128)S(1)} collective-permute-done((f32[1,1,68,256]{3,2,1,0:T(8,128)S(1)}, f32[1,1,68,256]{3,2,1,0:T(8,128)S(1)}, u32[]{:S(2)}, u32[]{:S(2)}) %collective-permute-start.2) | collective-permute-done | bytes 69664 | tf_op jit(solution)/shard_map/ppermute | solution.py:22
  194.4 6.3 %collective-permute-done.4 = f32[1,3,68,256]{3,2,1,0:T(8,128)S(1)} collective-permute-done((f32[1,3,68,256]{3,2,1,0:T(8,128)S(1)}, f32[1,3,68,256]{3,2,1,0:T(8,128)S(1)}, u32[]{:S(2)}, u32[]{:S(2)}) %collective-permute-start.4) | collective-permute-done | bytes 208928 | tf_op jit(solution)/shard_map/ppermute | solution.py:22
  200.6 2.7 %collective-permute-done.5 = f32[1,3,68,256]{3,2,1,0:T(8,128)S(1)} collective-permute-done((f32[1,3,68,256]{3,2,1,0:T(8,128)S(1)}, f32[1,3,68,256]{3,2,1,0:T(8,128)S(1)}, u32[]{:S(2)}, u32[]{:S(2)}) %collective-permute-start.5) | collective-permute-done | bytes 208928 | tf_op jit(solution)/shard_map/ppermute | solution.py:25
  219.2 23.5 %all_to_all.30 = f32[64,3,16,1,128]{4,2,1,3,0:T(8,128)S(1)} all-to-all(f32[64,3,16,1,128]{4,2,1,3,0:T(8,128)S(1)} %bitcast.263), channel_id=1, replica_groups=mesh['member'=8,'strip'=4] {'member'}, dimensions={0} | all-to-all | bytes 3145728 | tf_op jit(solution)/shard_map/all_to_all | solution.py:170
  (156 shorter events, 60.4 us)
Async XLA Ops:
  1.7 14.6 %collective-permute-start = (f32[8,3,3,1024]{3,2,0,1:T(4,128)S(1)}, f32[8,3,3,1024]{3,2,0,1:T(4,128)S(1)}, u32[]{:S(2)}, u32[]{:S(2)}) collective-permute-start(f32[8,3,3,1024]{3,2,0,1:T(4,128)S(1)} %get-tuple-element.91), channel_id=1, source_target_pairs={{1,0},{2,1},{3,2},{0,3},{5,4},{6,5},{7,6},{4,7},{9,8},{10,9},{11,1... | collective-permute-start | bytes 884744 | tf_op jit(solution)/shard_map/while/body/eval_jaxpr/ppermute | solution.py:25
  6.8 17.7 %collective-permute-start.1 = (f32[8,3,3,1024]{3,2,0,1:T(4,128)S(1)}, f32[8,3,3,1024]{3,2,0,1:T(4,128)S(1)}, u32[]{:S(2)}, u32[]{:S(2)}) collective-permute-start(f32[8,3,3,1024]{3,2,0,1:T(4,128)S(1)} %get-tuple-element.92), channel_id=1, source_target_pairs={{0,1},{1,2},{2,3},{3,0},{4,5},{5,6},{6,7},{7,4},{8,9},{9,10},{10,1... | collective-permute-start | bytes 884744 | tf_op jit(solution)/shard_map/while/body/eval_jaxpr/ppermute | solution.py:22
  24.9 1.4 copy-start
  41.8 18.5 %collective-permute-start = (f32[8,3,3,1024]{3,2,0,1:T(4,128)S(1)}, f32[8,3,3,1024]{3,2,0,1:T(4,128)S(1)}, u32[]{:S(2)}, u32[]{:S(2)}) collective-permute-start(f32[8,3,3,1024]{3,2,0,1:T(4,128)S(1)} %get-tuple-element.91), channel_id=1, source_target_pairs={{1,0},{2,1},{3,2},{0,3},{5,4},{6,5},{7,6},{4,7},{9,8},{10,9},{11,1... | collective-permute-start | bytes 884744 | tf_op jit(solution)/shard_map/while/body/eval_jaxpr/ppermute | solution.py:25
  43.6 16.7 %collective-permute-start.1 = (f32[8,3,3,1024]{3,2,0,1:T(4,128)S(1)}, f32[8,3,3,1024]{3,2,0,1:T(4,128)S(1)}, u32[]{:S(2)}, u32[]{:S(2)}) collective-permute-start(f32[8,3,3,1024]{3,2,0,1:T(4,128)S(1)} %get-tuple-element.92), channel_id=1, source_target_pairs={{0,1},{1,2},{2,3},{3,0},{4,5},{5,6},{6,7},{7,4},{8,9},{9,10},{10,1... | collective-permute-start | bytes 884744 | tf_op jit(solution)/shard_map/while/body/eval_jaxpr/ppermute | solution.py:22
  60.6 1.4 copy-start
  77.5 12.1 %collective-permute-start = (f32[8,3,3,1024]{3,2,0,1:T(4,128)S(1)}, f32[8,3,3,1024]{3,2,0,1:T(4,128)S(1)}, u32[]{:S(2)}, u32[]{:S(2)}) collective-permute-start(f32[8,3,3,1024]{3,2,0,1:T(4,128)S(1)} %get-tuple-element.91), channel_id=1, source_target_pairs={{1,0},{2,1},{3,2},{0,3},{5,4},{6,5},{7,6},{4,7},{9,8},{10,9},{11,1... | collective-permute-start | bytes 884744 | tf_op jit(solution)/shard_map/while/body/eval_jaxpr/ppermute | solution.py:25
  80.1 18.7 %collective-permute-start.1 = (f32[8,3,3,1024]{3,2,0,1:T(4,128)S(1)}, f32[8,3,3,1024]{3,2,0,1:T(4,128)S(1)}, u32[]{:S(2)}, u32[]{:S(2)}) collective-permute-start(f32[8,3,3,1024]{3,2,0,1:T(4,128)S(1)} %get-tuple-element.92), channel_id=1, source_target_pairs={{0,1},{1,2},{2,3},{3,0},{4,5},{5,6},{6,7},{7,4},{8,9},{9,10},{10,1... | collective-permute-start | bytes 884744 | tf_op jit(solution)/shard_map/while/body/eval_jaxpr/ppermute | solution.py:22
  99.2 1.4 copy-start
  116.0 11.3 %collective-permute-start = (f32[8,3,3,1024]{3,2,0,1:T(4,128)S(1)}, f32[8,3,3,1024]{3,2,0,1:T(4,128)S(1)}, u32[]{:S(2)}, u32[]{:S(2)}) collective-permute-start(f32[8,3,3,1024]{3,2,0,1:T(4,128)S(1)} %get-tuple-element.91), channel_id=1, source_target_pairs={{1,0},{2,1},{3,2},{0,3},{5,4},{6,5},{7,6},{4,7},{9,8},{10,9},{11,1... | collective-permute-start | bytes 884744 | tf_op jit(solution)/shard_map/while/body/eval_jaxpr/ppermute | solution.py:25
  117.8 17.6 %collective-permute-start.1 = (f32[8,3,3,1024]{3,2,0,1:T(4,128)S(1)}, f32[8,3,3,1024]{3,2,0,1:T(4,128)S(1)}, u32[]{:S(2)}, u32[]{:S(2)}) collective-permute-start(f32[8,3,3,1024]{3,2,0,1:T(4,128)S(1)} %get-tuple-element.92), channel_id=1, source_target_pairs={{0,1},{1,2},{2,3},{3,0},{4,5},{5,6},{6,7},{7,4},{8,9},{9,10},{10,1... | collective-permute-start | bytes 884744 | tf_op jit(solution)/shard_map/while/body/eval_jaxpr/ppermute | solution.py:22
  135.8 1.4 copy-start
  155.0 5.2 %copy-start.1 = (s32[1,1,256]{2,1,0:T(1,128)S(1)}, s32[1,1,256]{2,1,0:T(1,128)}, u32[]{:S(2)}) copy-start(s32[1,1,256]{2,1,0:T(1,128)} %param.10) | copy-start | bytes 3076
  155.0 5.2 %copy-start.3 = (f32[1,1,256]{2,1,0:T(1,128)S(1)}, f32[1,1,256]{2,1,0:T(1,128)}, u32[]{:S(2)}) copy-start(f32[1,1,256]{2,1,0:T(1,128)} %param.12) | copy-start | bytes 3076
  155.0 24.9 %all-to-all-start = ((f32[8,3,16,8,128]{4,0,2,1,3:T(8,128)}), f32[8,3,16,8,128]{4,0,2,1,3:T(8,128)S(1)}, u32[]{:S(2)}, u32[]{:S(2)}) async-start(f32[8,3,16,8,128]{4,0,2,1,3:T(8,128)} %copy.23), calls=%async_computation | async-start | bytes 3145728 | tf_op jit(solution)/shard_map/all_to_all | solution.py:162
  179.9 5.0 %copy-start.2 = (f32[1,1,256]{2,1,0:T(1,128)S(1)}, f32[1,1,256]{2,1,0:T(1,128)}, u32[]{:S(2)}) copy-start(f32[1,1,256]{2,1,0:T(1,128)} %param.11) | copy-start | bytes 3076
  184.9 5.5 %collective-permute-start.2 = (f32[1,1,68,256]{3,2,1,0:T(8,128)S(1)}, f32[1,1,68,256]{3,2,1,0:T(8,128)S(1)}, u32[]{:S(2)}, u32[]{:S(2)}) collective-permute-start(f32[1,1,68,256]{3,2,1,0:T(8,128)S(1)} %bitcast.265), channel_id=1, source_target_pairs={{0,4},{4,8},{8,12},{12,16},{16,20},{20,24},{24,28},{28,0},{1,5},{5... | collective-permute-start | bytes 208904 | tf_op jit(solution)/shard_map/ppermute | solution.py:22
  185.0 5.5 %collective-permute-start.3 = (f32[1,1,68,256]{3,2,1,0:T(8,128)S(1)}, f32[1,1,68,256]{3,2,1,0:T(8,128)S(1)}, u32[]{:S(2)}, u32[]{:S(2)}) collective-permute-start(f32[1,1,68,256]{3,2,1,0:T(8,128)S(1)} %bitcast.266), channel_id=1, source_target_pairs={{4,0},{8,4},{12,8},{16,12},{20,16},{24,20},{28,24},{0,28},{5,1},{9... | collective-permute-start | bytes 208904 | tf_op jit(solution)/shard_map/ppermute | solution.py:25
  190.5 10.2 %collective-permute-start.4 = (f32[1,3,68,256]{3,2,1,0:T(8,128)S(1)}, f32[1,3,68,256]{3,2,1,0:T(8,128)S(1)}, u32[]{:S(2)}, u32[]{:S(2)}) collective-permute-start(f32[1,3,68,256]{3,2,1,0:T(8,128)S(1)} %pad_maximum_fusion.3), channel_id=1, source_target_pairs={{0,1},{1,2},{2,3},{3,0},{4,5},{5,6},{6,7},{7,4},{8,9},{9,10},{10,1... | collective-permute-start | bytes 626696 | tf_op jit(solution)/shard_map/ppermute | solution.py:22
  192.3 11.0 %collective-permute-start.5 = (f32[1,3,68,256]{3,2,1,0:T(8,128)S(1)}, f32[1,3,68,256]{3,2,1,0:T(8,128)S(1)}, u32[]{:S(2)}, u32[]{:S(2)}) collective-permute-start(f32[1,3,68,256]{3,2,1,0:T(8,128)S(1)} %pad_maximum_fusion.3), channel_id=1, source_target_pairs={{1,0},{2,1},{3,2},{0,3},{5,4},{6,5},{7,6},{4,7},{9,8},{10,9},{11,1... | collective-permute-start | bytes 626696 | tf_op jit(solution)/shard_map/ppermute | solution.py:25
where the time goes:
time: 246 us; the launch traced here: 245 us
  waiting for transfers between devices  101 us (41%)
  other arithmetic  48.9 us (20%)
  local copies, waits for them, and re-layouts  32.3 us (13%)
  blocking collectives  23.5 us (10%)
  starting transfers between devices  22.3 us (9%)
  matrix products  13.3 us (5%)
  between operations  2.7 us (1%)
    ppermute x6, waiting for transfers between devices, with_halo(): lax.ppermute(lax.slice_in_dim(block, 0, width, axis=dim), axis, backward)  47.3 us
    ppermute x6, waiting for transfers between devices, with_halo(): lax.ppermute(lax.slice_in_dim(block, block.shape[dim] - width, None, axis...  34.5 us
    all_to_all x1, blocking collectives, on_device(): lax.all_to_all(outgoing, 'member', split_axis=0, concat_axis=3, tiled=True)  23.5 us
    mul x12, other arithmetic, advance_once(): flux_x = column_depth * flow_x  22.8 us
    all_to_all x1, waiting for transfers between devices, on_device(): lax.all_to_all(by_block, 'member', split_axis=3, concat_axis=0, tiled=True)  19.6 us
    ppermute x6, starting transfers between devices, with_halo(): lax.ppermute(lax.slice_in_dim(block, 0, width, axis=dim), axis, backward)  16 us
    mul x8, other arithmetic, advance_once(): flux_y = column_depth * flow_y  13.6 us
    concatenate x4, local copies, waits for them, and re-layouts, strip_block(): jnp.concatenate([padded[..., -halo_depth:], padded, padded[..., :halo_dep...  13 us
  transfers between devices with their start and end apart: 13, of which 11 were waited for; matrix products, arithmetic and copies ran while one was open for 0% of the time, Pallas kernels for 0%

commit v1 on v0

--- a/solution.py
+++ b/solution.py
@@ -159,7 +159,15 @@
 
     current_state = lax.fori_loop(0, rounds, strip_round, sample_fields)
     by_block = current_state.reshape(own_members, fields, row_count, blocks, region_cols)
-    current_state = lax.all_to_all(by_block, "member", split_axis=3, concat_axis=0, tiled=True)
+    ways, here = (lax.axis_size("member"), lax.axis_index("member"))
+    width_2 = by_block.shape[3] // ways
+    turned = jnp.roll(by_block, -here * width_2, axis=3)
+    got = [lax.slice_in_dim(turned, 0, width_2, axis=3)]
+    for far in range(1, ways):
+        sent = lax.slice_in_dim(turned, far * width_2, (far + 1) * width_2, axis=3)
+        got.append(lax.ppermute(sent, "member", [(d, (d + far) % ways) for d in range(ways)]))
+    line = jnp.concatenate(got[::-1], axis=0)
+    current_state = jnp.roll(line, (here + 1) * got[0].shape[0], axis=0)
     region = current_state.reshape(sample_collection, fields * row_count * region_cols)
     packed = observe(
         region, report_cells[0, 0], report_values[0, 0], report_errors[0, 0], report_counts[0, 0]

time: 246 us -> 243 us (0.988)
  waiting for transfers between devices: 101 us -> 95.4 us
    all_to_all x1 -> x0, waiting for transfers between devices: 19.6 us -> none  [on_device(): lax.all_to_all(by_block, 'member', split_axis=3, concat_axis=0, tiled=True)]
    ppermute x0 -> x7, waiting for transfers between devices: none -> 13.5 us  [on_device(): lax.ppermute(sent, 'member', [(d, (d + far) % ways) for d in range(ways)])]
    ppermute x0 -> x7, starting transfers between devices: none -> 5.93 us  [on_device(): lax.ppermute(sent, 'member', [(d, (d + far) % ways) for d in range(ways)])]
    all_to_all x1 -> x0, starting transfers between devices: 3.85 us -> none  [on_device(): lax.all_to_all(by_block, 'member', split_axis=3, concat_axis=0, tiled=True)]
    ppermute x6, starting transfers between devices: 16 us -> 13.3 us  [with_halo(): lax.ppermute(lax.slice_in_dim(block, 0, width, axis=dim), axis, backward)]
  transfers between devices with their start and end apart: 13 -> 19, of which waited for: 11 -> 14; matrix products, arithmetic and copies ran while one was open for 0% -> 1% of each run, Pallas kernels for 0% -> 0%
where the time goes in v1:
time: 243 us; the launch traced here: 242 us
  waiting for transfers between devices  95.4 us (39%)
  other arithmetic  50.9 us (21%)
  local copies, waits for them, and re-layouts  31.8 us (13%)
  blocking collectives  25.3 us (10%)
  starting transfers between devices  22.3 us (9%)
  matrix products  13.3 us (5%)
  between operations  2.88 us (1%)
    ppermute x6, waiting for transfers between devices, with_halo(): lax.ppermute(lax.slice_in_dim(block, 0, width, axis=dim), axis, backward)  48.6 us
    ppermute x6, waiting for transfers between devices, with_halo(): lax.ppermute(lax.slice_in_dim(block, block.shape[dim] - width, None, axis...  33.2 us
    all_to_all x1, blocking collectives, on_device(): lax.all_to_all(outgoing, 'member', split_axis=0, concat_axis=3, tiled=True)  25.3 us
    mul x12, other arithmetic, advance_once(): flux_x = column_depth * flow_x  22.8 us
    mul x8, other arithmetic, advance_once(): flux_y = column_depth * flow_y  13.6 us
    ppermute x7, waiting for transfers between devices, on_device(): lax.ppermute(sent, 'member', [(d, (d + far) % ways) for d in range(ways)])  13.5 us
    ppermute x6, starting transfers between devices, with_halo(): lax.ppermute(lax.slice_in_dim(block, 0, width, axis=dim), axis, backward)  13.3 us
    concatenate x4, local copies, waits for them, and re-layouts, strip_block(): jnp.concatenate([padded[..., -halo_depth:], padded, padded[..., :halo_dep...  13 us
  transfers between devices with their start and end apart: 19, of which 14 were waited for; matrix products, arithmetic and copies ran while one was open for 1% of the time, Pallas kernels for 0%

profile of v1, /device:TPU:0, one launch (start us, length us, event | category | flops | bytes accessed | tf_op | source)
XLA Modules:
  0.0 242.3 jit_solution(199056094178455263)
XLA Ops:
  1.5 150.9 %while.10 = (s32[]{:T(128)}, f32[8,3,16,1024]{3,2,0,1:T(8,128)S(1)}, s32[]{:T(128)}) while((s32[]{:T(128)}, f32[8,3,16,1024]{3,2,0,1:T(8,128)S(1)}, s32[]{:T(128)}) %tuple.63), condition=%wide.region_1.0_spmd, body=%wide.region_0.0_spmd.sunk | while | flops 20949056 | bytes 80089624 | solution.py:160
  1.7 5.1 %collective-permute-start = (f32[8,3,3,1024]{3,2,0,1:T(4,128)S(1)}, f32[8,3,3,1024]{3,2,0,1:T(4,128)S(1)}, u32[]{:S(2)}, u32[]{:S(2)}) collective-permute-start(f32[8,3,3,1024]{3,2,0,1:T(4,128)S(1)} %get-tuple-element.100), channel_id=1, source_target_pairs={{1,0},{2,1},{3,2},{0,3},{5,4},{6,5},{7,6},{4,7},{9,8},{10,9},{11,1... | collective-permute-start | bytes 884744 | tf_op jit(solution)/shard_map/while/body/eval_jaxpr/ppermute | solution.py:25
  6.8 9.5 %collective-permute-done = f32[8,3,3,1024]{3,2,0,1:T(4,128)S(1)} collective-permute-done((f32[8,3,3,1024]{3,2,0,1:T(4,128)S(1)}, f32[8,3,3,1024]{3,2,0,1:T(4,128)S(1)}, u32[]{:S(2)}, u32[]{:S(2)}) %collective-permute-start) | collective-permute-done | bytes 294944 | tf_op jit(solution)/shard_map/while/body/eval_jaxpr/ppermute | solution.py:25
  16.3 8.2 %collective-permute-done.1 = f32[8,3,3,1024]{3,2,0,1:T(4,128)S(1)} collective-permute-done((f32[8,3,3,1024]{3,2,0,1:T(4,128)S(1)}, f32[8,3,3,1024]{3,2,0,1:T(4,128)S(1)}, u32[]{:S(2)}, u32[]{:S(2)}) %collective-permute-start.1) | collective-permute-done | bytes 294944 | tf_op jit(solution)/shard_map/while/body/eval_jaxpr/ppermute | solution.py:22
  26.4 3.2 %concatenate.31 = f32[8,3,22,1030]{3,2,0,1:T(8,128)S(1)} concatenate(f32[8,3,22,3]{3,2,0,1:T(8,128)S(1)} %get-tuple-element.102, f32[8,3,22,1024]{3,2,0,1:T(8,128)} %copy-done, f32[8,3,22,3]{3,2,0,1:T(8,128)S(1)} %get-tuple-element.103), dimensions={3} | concatenate | bytes 4350720 | tf_op jit(solution)/shard_map/while/body/eval_jaxpr/concatenate | solution.py:141
  29.9 2.8 %add_multiply_fusion.12 = (f32[8,20,1028]{2,1,0:T(8,128)S(1)}, f32[8,20,1028]{2,1,0:T(8,128)S(1)}, f32[8,20,1028]{2,1,0:T(8,128)S(1)}) fusion(f32[8,22,1030]{2,1,0:T(8,128)S(1)} %get-tuple-element.104, f32[8,22,1030]{2,1,0:T(8,128)S(1)} %get-tuple-element.105, f32[8,22,1030]{2,1,0:T(8,128)S(1)} %get-tuple-element.106, ...), kind=kLoop, calls=%fused_computation.23.clone.1 | loop fusion | flops 4276480 | bytes 11184640 | tf_op jit(solution)/shard_map/while/body/eval_jaxpr/mul | solution.py:59
  34.4 2.8 %add_multiply_fusion.14 = (f32[8,18,1026]{2,1,0:T(8,128)S(1)}, f32[8,18,1026]{2,1,0:T(8,128)S(1)}, f32[8,18,1026]{2,1,0:T(8,128)S(1)}) fusion(f32[8,20,1028]{2,1,0:T(8,128)S(1)} %get-tuple-element.110, f32[8,20,1028]{2,1,0:T(8,128)S(1)} %get-tuple-element.111, f32[8,20,1028]{2,1,0:T(8,128)S(1)} %get-tuple-element.109, ...), kind=kLoop, calls=%fused_computation.21.clone.1 | loop fusion | flops 3841344 | bytes 10046592 | tf_op jit(solution)/shard_map/while/body/eval_jaxpr/mul | solution.py:59
  43.8 16.4 %collective-permute-done = f32[8,3,3,1024]{3,2,0,1:T(4,128)S(1)} collective-permute-done((f32[8,3,3,1024]{3,2,0,1:T(4,128)S(1)}, f32[8,3,3,1024]{3,2,0,1:T(4,128)S(1)}, u32[]{:S(2)}, u32[]{:S(2)}) %collective-permute-start) | collective-permute-done | bytes 294944 | tf_op jit(solution)/shard_map/while/body/eval_jaxpr/ppermute | solution.py:25
  62.0 3.2 %concatenate.31 = f32[8,3,22,1030]{3,2,0,1:T(8,128)S(1)} concatenate(f32[8,3,22,3]{3,2,0,1:T(8,128)S(1)} %get-tuple-element.102, f32[8,3,22,1024]{3,2,0,1:T(8,128)} %copy-done, f32[8,3,22,3]{3,2,0,1:T(8,128)S(1)} %get-tuple-element.103), dimensions={3} | concatenate | bytes 4350720 | tf_op jit(solution)/shard_map/while/body/eval_jaxpr/concatenate | solution.py:141
  65.6 2.8 %add_multiply_fusion.12 = (f32[8,20,1028]{2,1,0:T(8,128)S(1)}, f32[8,20,1028]{2,1,0:T(8,128)S(1)}, f32[8,20,1028]{2,1,0:T(8,128)S(1)}) fusion(f32[8,22,1030]{2,1,0:T(8,128)S(1)} %get-tuple-element.104, f32[8,22,1030]{2,1,0:T(8,128)S(1)} %get-tuple-element.105, f32[8,22,1030]{2,1,0:T(8,128)S(1)} %get-tuple-element.106, ...), kind=kLoop, calls=%fused_computation.23.clone.1 | loop fusion | flops 4276480 | bytes 11184640 | tf_op jit(solution)/shard_map/while/body/eval_jaxpr/mul | solution.py:59
  70.1 2.8 %add_multiply_fusion.14 = (f32[8,18,1026]{2,1,0:T(8,128)S(1)}, f32[8,18,1026]{2,1,0:T(8,128)S(1)}, f32[8,18,1026]{2,1,0:T(8,128)S(1)}) fusion(f32[8,20,1028]{2,1,0:T(8,128)S(1)} %get-tuple-element.110, f32[8,20,1028]{2,1,0:T(8,128)S(1)} %get-tuple-element.111, f32[8,20,1028]{2,1,0:T(8,128)S(1)} %get-tuple-element.109, ...), kind=kLoop, calls=%fused_computation.21.clone.1 | loop fusion | flops 3841344 | bytes 10046592 | tf_op jit(solution)/shard_map/while/body/eval_jaxpr/mul | solution.py:59
  77.4 2.6 %collective-permute-start = (f32[8,3,3,1024]{3,2,0,1:T(4,128)S(1)}, f32[8,3,3,1024]{3,2,0,1:T(4,128)S(1)}, u32[]{:S(2)}, u32[]{:S(2)}) collective-permute-start(f32[8,3,3,1024]{3,2,0,1:T(4,128)S(1)} %get-tuple-element.100), channel_id=1, source_target_pairs={{1,0},{2,1},{3,2},{0,3},{5,4},{6,5},{7,6},{4,7},{9,8},{10,9},{11,1... | collective-permute-start | bytes 884744 | tf_op jit(solution)/shard_map/while/body/eval_jaxpr/ppermute | solution.py:25
  80.0 9.5 %collective-permute-done = f32[8,3,3,1024]{3,2,0,1:T(4,128)S(1)} collective-permute-done((f32[8,3,3,1024]{3,2,0,1:T(4,128)S(1)}, f32[8,3,3,1024]{3,2,0,1:T(4,128)S(1)}, u32[]{:S(2)}, u32[]{:S(2)}) %collective-permute-start) | collective-permute-done | bytes 294944 | tf_op jit(solution)/shard_map/while/body/eval_jaxpr/ppermute | solution.py:25
  89.5 9.2 %collective-permute-done.1 = f32[8,3,3,1024]{3,2,0,1:T(4,128)S(1)} collective-permute-done((f32[8,3,3,1024]{3,2,0,1:T(4,128)S(1)}, f32[8,3,3,1024]{3,2,0,1:T(4,128)S(1)}, u32[]{:S(2)}, u32[]{:S(2)}) %collective-permute-start.1) | collective-permute-done | bytes 294944 | tf_op jit(solution)/shard_map/while/body/eval_jaxpr/ppermute | solution.py:22
  100.5 3.2 %concatenate.31 = f32[8,3,22,1030]{3,2,0,1:T(8,128)S(1)} concatenate(f32[8,3,22,3]{3,2,0,1:T(8,128)S(1)} %get-tuple-element.102, f32[8,3,22,1024]{3,2,0,1:T(8,128)} %copy-done, f32[8,3,22,3]{3,2,0,1:T(8,128)S(1)} %get-tuple-element.103), dimensions={3} | concatenate | bytes 4350720 | tf_op jit(solution)/shard_map/while/body/eval_jaxpr/concatenate | solution.py:141
  104.1 2.8 %add_multiply_fusion.12 = (f32[8,20,1028]{2,1,0:T(8,128)S(1)}, f32[8,20,1028]{2,1,0:T(8,128)S(1)}, f32[8,20,1028]{2,1,0:T(8,128)S(1)}) fusion(f32[8,22,1030]{2,1,0:T(8,128)S(1)} %get-tuple-element.104, f32[8,22,1030]{2,1,0:T(8,128)S(1)} %get-tuple-element.105, f32[8,22,1030]{2,1,0:T(8,128)S(1)} %get-tuple-element.106, ...), kind=kLoop, calls=%fused_computation.23.clone.1 | loop fusion | flops 4276480 | bytes 11184640 | tf_op jit(solution)/shard_map/while/body/eval_jaxpr/mul | solution.py:59
  108.6 2.8 %add_multiply_fusion.14 = (f32[8,18,1026]{2,1,0:T(8,128)S(1)}, f32[8,18,1026]{2,1,0:T(8,128)S(1)}, f32[8,18,1026]{2,1,0:T(8,128)S(1)}) fusion(f32[8,20,1028]{2,1,0:T(8,128)S(1)} %get-tuple-element.110, f32[8,20,1028]{2,1,0:T(8,128)S(1)} %get-tuple-element.111, f32[8,20,1028]{2,1,0:T(8,128)S(1)} %get-tuple-element.109, ...), kind=kLoop, calls=%fused_computation.21.clone.1 | loop fusion | flops 3841344 | bytes 10046592 | tf_op jit(solution)/shard_map/while/body/eval_jaxpr/mul | solution.py:59
  117.9 9.2 %collective-permute-done = f32[8,3,3,1024]{3,2,0,1:T(4,128)S(1)} collective-permute-done((f32[8,3,3,1024]{3,2,0,1:T(4,128)S(1)}, f32[8,3,3,1024]{3,2,0,1:T(4,128)S(1)}, u32[]{:S(2)}, u32[]{:S(2)}) %collective-permute-start) | collective-permute-done | bytes 294944 | tf_op jit(solution)/shard_map/while/body/eval_jaxpr/ppermute | solution.py:25
  127.2 8.1 %collective-permute-done.1 = f32[8,3,3,1024]{3,2,0,1:T(4,128)S(1)} collective-permute-done((f32[8,3,3,1024]{3,2,0,1:T(4,128)S(1)}, f32[8,3,3,1024]{3,2,0,1:T(4,128)S(1)}, u32[]{:S(2)}, u32[]{:S(2)}) %collective-permute-start.1) | collective-permute-done | bytes 294944 | tf_op jit(solution)/shard_map/while/body/eval_jaxpr/ppermute | solution.py:22
  137.1 3.2 %concatenate.31 = f32[8,3,22,1030]{3,2,0,1:T(8,128)S(1)} concatenate(f32[8,3,22,3]{3,2,0,1:T(8,128)S(1)} %get-tuple-element.102, f32[8,3,22,1024]{3,2,0,1:T(8,128)} %copy-done, f32[8,3,22,3]{3,2,0,1:T(8,128)S(1)} %get-tuple-element.103), dimensions={3} | concatenate | bytes 4350720 | tf_op jit(solution)/shard_map/while/body/eval_jaxpr/concatenate | solution.py:141
  140.7 2.8 %add_multiply_fusion.12 = (f32[8,20,1028]{2,1,0:T(8,128)S(1)}, f32[8,20,1028]{2,1,0:T(8,128)S(1)}, f32[8,20,1028]{2,1,0:T(8,128)S(1)}) fusion(f32[8,22,1030]{2,1,0:T(8,128)S(1)} %get-tuple-element.104, f32[8,22,1030]{2,1,0:T(8,128)S(1)} %get-tuple-element.105, f32[8,22,1030]{2,1,0:T(8,128)S(1)} %get-tuple-element.106, ...), kind=kLoop, calls=%fused_computation.23.clone.1 | loop fusion | flops 4276480 | bytes 11184640 | tf_op jit(solution)/shard_map/while/body/eval_jaxpr/mul | solution.py:59
  145.1 2.8 %add_multiply_fusion.14 = (f32[8,18,1026]{2,1,0:T(8,128)S(1)}, f32[8,18,1026]{2,1,0:T(8,128)S(1)}, f32[8,18,1026]{2,1,0:T(8,128)S(1)}) fusion(f32[8,20,1028]{2,1,0:T(8,128)S(1)} %get-tuple-element.110, f32[8,20,1028]{2,1,0:T(8,128)S(1)} %get-tuple-element.111, f32[8,20,1028]{2,1,0:T(8,128)S(1)} %get-tuple-element.109, ...), kind=kLoop, calls=%fused_computation.21.clone.1 | loop fusion | flops 3841344 | bytes 10046592 | tf_op jit(solution)/shard_map/while/body/eval_jaxpr/mul | solution.py:59
  163.3 2.5 %collective-permute-done.3 = f32[8,3,16,1,128]{4,2,1,0,3:T(8,128)S(1)} collective-permute-done((f32[8,3,16,1,128]{4,2,1,0,3:T(8,128)}, f32[8,3,16,1,128]{4,2,1,0,3:T(8,128)S(1)}, u32[]{:S(2)}, u32[]{:S(2)}) %collective-permute-start.3) | collective-permute-done | bytes 196640 | tf_op jit(solution)/shard_map/ppermute | solution.py:168
  166.0 10.8 %collective-permute-done.5 = f32[8,3,16,1,128]{4,2,1,0,3:T(8,128)S(1)} collective-permute-done((f32[8,3,16,1,128]{4,2,1,0,3:T(8,128)S(1)}, f32[8,3,16,1,128]{4,2,1,0,3:T(8,128)S(1)}, u32[]{:S(2)}, u32[]{:S(2)}) %collective-permute-start.5) | collective-permute-done | bytes 196640 | tf_op jit(solution)/shard_map/ppermute | solution.py:168
  177.6 2.2 copy.27
  179.8 2.6 %gather_fusion = f32[256,64]{1,0:T(8,128)S(1)} fusion(f32[64,6144]{0,1:T(8,128)} %copy.27, s32[1024]{0:T(1024)S(1)} %pad_clamp_fusion), kind=kCustom, calls=%fused_computation | custom fusion | bytes 132096 | tf_op jit(solution)/shard_map/jit(_take)/gather | solution.py:90
  183.2 2.0 collective-permute-done.10
  185.2 2.3 collective-permute-done.9
  187.5 2.0 collective-permute-start.11
  191.4 5.5 %collective-permute-done.11 = f32[1,3,68,256]{3,2,1,0:T(8,128)S(1)} collective-permute-done((f32[1,3,68,256]{3,2,1,0:T(8,128)S(1)}, f32[1,3,68,256]{3,2,1,0:T(8,128)S(1)}, u32[]{:S(2)}, u32[]{:S(2)}) %collective-permute-start.11) | collective-permute-done | bytes 208928 | tf_op jit(solution)/shard_map/ppermute | solution.py:22
  196.9 2.0 collective-permute-done.12
  214.8 25.3 %all_to_all.15 = f32[64,3,16,1,128]{4,2,1,3,0:T(8,128)S(1)} all-to-all(f32[64,3,16,1,128]{4,2,1,3,0:T(8,128)S(1)} %bitcast.259), channel_id=1, replica_groups=mesh['member'=8,'strip'=4] {'member'}, dimensions={0} | all-to-all | bytes 3145728 | tf_op jit(solution)/shard_map/all_to_all | solution.py:178
  (189 shorter events, 68.6 us)
Async XLA Ops:
  1.7 14.6 %collective-permute-start = (f32[8,3,3,1024]{3,2,0,1:T(4,128)S(1)}, f32[8,3,3,1024]{3,2,0,1:T(4,128)S(1)}, u32[]{:S(2)}, u32[]{:S(2)}) collective-permute-start(f32[8,3,3,1024]{3,2,0,1:T(4,128)S(1)} %get-tuple-element.100), channel_id=1, source_target_pairs={{1,0},{2,1},{3,2},{0,3},{5,4},{6,5},{7,6},{4,7},{9,8},{10,9},{11,1... | collective-permute-start | bytes 884744 | tf_op jit(solution)/shard_map/while/body/eval_jaxpr/ppermute | solution.py:25
  6.8 17.7 %collective-permute-start.1 = (f32[8,3,3,1024]{3,2,0,1:T(4,128)S(1)}, f32[8,3,3,1024]{3,2,0,1:T(4,128)S(1)}, u32[]{:S(2)}, u32[]{:S(2)}) collective-permute-start(f32[8,3,3,1024]{3,2,0,1:T(4,128)S(1)} %get-tuple-element.101), channel_id=1, source_target_pairs={{0,1},{1,2},{2,3},{3,0},{4,5},{5,6},{6,7},{7,4},{8,9},{9,10},{10,1... | collective-permute-start | bytes 884744 | tf_op jit(solution)/shard_map/while/body/eval_jaxpr/ppermute | solution.py:22
  24.9 1.4 copy-start
  41.7 18.5 %collective-permute-start = (f32[8,3,3,1024]{3,2,0,1:T(4,128)S(1)}, f32[8,3,3,1024]{3,2,0,1:T(4,128)S(1)}, u32[]{:S(2)}, u32[]{:S(2)}) collective-permute-start(f32[8,3,3,1024]{3,2,0,1:T(4,128)S(1)} %get-tuple-element.100), channel_id=1, source_target_pairs={{1,0},{2,1},{3,2},{0,3},{5,4},{6,5},{7,6},{4,7},{9,8},{10,9},{11,1... | collective-permute-start | bytes 884744 | tf_op jit(solution)/shard_map/while/body/eval_jaxpr/ppermute | solution.py:25
  43.5 16.7 %collective-permute-start.1 = (f32[8,3,3,1024]{3,2,0,1:T(4,128)S(1)}, f32[8,3,3,1024]{3,2,0,1:T(4,128)S(1)}, u32[]{:S(2)}, u32[]{:S(2)}) collective-permute-start(f32[8,3,3,1024]{3,2,0,1:T(4,128)S(1)} %get-tuple-element.101), channel_id=1, source_target_pairs={{0,1},{1,2},{2,3},{3,0},{4,5},{5,6},{6,7},{7,4},{8,9},{9,10},{10,1... | collective-permute-start | bytes 884744 | tf_op jit(solution)/shard_map/while/body/eval_jaxpr/ppermute | solution.py:22
  60.6 1.4 copy-start
  77.4 12.1 %collective-permute-start = (f32[8,3,3,1024]{3,2,0,1:T(4,128)S(1)}, f32[8,3,3,1024]{3,2,0,1:T(4,128)S(1)}, u32[]{:S(2)}, u32[]{:S(2)}) collective-permute-start(f32[8,3,3,1024]{3,2,0,1:T(4,128)S(1)} %get-tuple-element.100), channel_id=1, source_target_pairs={{1,0},{2,1},{3,2},{0,3},{5,4},{6,5},{7,6},{4,7},{9,8},{10,9},{11,1... | collective-permute-start | bytes 884744 | tf_op jit(solution)/shard_map/while/body/eval_jaxpr/ppermute | solution.py:25
  80.0 18.7 %collective-permute-start.1 = (f32[8,3,3,1024]{3,2,0,1:T(4,128)S(1)}, f32[8,3,3,1024]{3,2,0,1:T(4,128)S(1)}, u32[]{:S(2)}, u32[]{:S(2)}) collective-permute-start(f32[8,3,3,1024]{3,2,0,1:T(4,128)S(1)} %get-tuple-element.101), channel_id=1, source_target_pairs={{0,1},{1,2},{2,3},{3,0},{4,5},{5,6},{6,7},{7,4},{8,9},{9,10},{10,1... | collective-permute-start | bytes 884744 | tf_op jit(solution)/shard_map/while/body/eval_jaxpr/ppermute | solution.py:22
  99.1 1.4 copy-start
  115.8 11.3 %collective-permute-start = (f32[8,3,3,1024]{3,2,0,1:T(4,128)S(1)}, f32[8,3,3,1024]{3,2,0,1:T(4,128)S(1)}, u32[]{:S(2)}, u32[]{:S(2)}) collective-permute-start(f32[8,3,3,1024]{3,2,0,1:T(4,128)S(1)} %get-tuple-element.100), channel_id=1, source_target_pairs={{1,0},{2,1},{3,2},{0,3},{5,4},{6,5},{7,6},{4,7},{9,8},{10,9},{11,1... | collective-permute-start | bytes 884744 | tf_op jit(solution)/shard_map/while/body/eval_jaxpr/ppermute | solution.py:25
  117.6 17.6 %collective-permute-start.1 = (f32[8,3,3,1024]{3,2,0,1:T(4,128)S(1)}, f32[8,3,3,1024]{3,2,0,1:T(4,128)S(1)}, u32[]{:S(2)}, u32[]{:S(2)}) collective-permute-start(f32[8,3,3,1024]{3,2,0,1:T(4,128)S(1)} %get-tuple-element.101), channel_id=1, source_target_pairs={{0,1},{1,2},{2,3},{3,0},{4,5},{5,6},{6,7},{7,4},{8,9},{9,10},{10,1... | collective-permute-start | bytes 884744 | tf_op jit(solution)/shard_map/while/body/eval_jaxpr/ppermute | solution.py:22
  135.6 1.4 copy-start
  153.1 5.6 %copy-start.1 = (s32[1,1,256]{2,1,0:T(1,128)S(1)}, s32[1,1,256]{2,1,0:T(1,128)}, u32[]{:S(2)}) copy-start(s32[1,1,256]{2,1,0:T(1,128)} %param.10) | copy-start | bytes 3076
  153.1 6.8 %copy-start.4 = (f32[1,1,256]{2,1,0:T(1,128)S(1)}, f32[1,1,256]{2,1,0:T(1,128)}, u32[]{:S(2)}) copy-start(f32[1,1,256]{2,1,0:T(1,128)} %param.12) | copy-start | bytes 3076
  154.3 7.5 %collective-permute-start.2 = (f32[8,3,16,1,128]{4,2,1,0,3:T(8,128)}, f32[8,3,16,1,128]{4,2,1,0,3:T(8,128)S(1)}, u32[]{:S(2)}, u32[]{:S(2)}) collective-permute-start(f32[8,3,16,1,128]{4,2,1,0,3:T(8,128)} %get-tuple-element.59), channel_id=1, source_target_pairs={{0,28},{4,0},{8,4},{12,8},{16,12},{20,16},{24,20},{28,24},{1,29},{... | collective-permute-start | bytes 589832 | tf_op jit(solution)/shard_map/ppermute | solution.py:168
  155.3 10.6 %collective-permute-start.3 = (f32[8,3,16,1,128]{4,2,1,0,3:T(8,128)}, f32[8,3,16,1,128]{4,2,1,0,3:T(8,128)S(1)}, u32[]{:S(2)}, u32[]{:S(2)}) collective-permute-start(f32[8,3,16,1,128]{4,2,1,0,3:T(8,128)} %get-tuple-element.58), channel_id=1, source_target_pairs={{0,24},{4,28},{8,0},{12,4},{16,8},{20,12},{24,16},{28,20},{1,25},{... | collective-permute-start | bytes 589832 | tf_op jit(solution)/shard_map/ppermute | solution.py:168
  156.7 9.3 %collective-permute-start.4 = (f32[8,3,16,1,128]{4,2,1,0,3:T(8,128)S(1)}, f32[8,3,16,1,128]{4,2,1,0,3:T(8,128)S(1)}, u32[]{:S(2)}, u32[]{:S(2)}) collective-permute-start(f32[8,3,16,1,128]{4,2,1,0,3:T(8,128)S(1)} %get-tuple-element.57), channel_id=1, source_target_pairs={{0,20},{4,24},{8,28},{12,0},{16,4},{20,8},{24,12},{28,16},{1,21},{... | collective-permute-start | bytes 589832 | tf_op jit(solution)/shard_map/ppermute | solution.py:168
  157.0 19.8 %collective-permute-start.5 = (f32[8,3,16,1,128]{4,2,1,0,3:T(8,128)S(1)}, f32[8,3,16,1,128]{4,2,1,0,3:T(8,128)S(1)}, u32[]{:S(2)}, u32[]{:S(2)}) collective-permute-start(f32[8,3,16,1,128]{4,2,1,0,3:T(8,128)S(1)} %get-tuple-element.56), channel_id=1, source_target_pairs={{0,16},{4,20},{8,24},{12,28},{16,0},{20,4},{24,8},{28,12},{1,17},{... | collective-permute-start | bytes 589832 | tf_op jit(solution)/shard_map/ppermute | solution.py:168
  158.6 18.3 %collective-permute-start.6 = (f32[8,3,16,1,128]{4,2,1,0,3:T(8,128)S(1)}, f32[8,3,16,1,128]{4,2,1,0,3:T(8,128)S(1)}, u32[]{:S(2)}, u32[]{:S(2)}) collective-permute-start(f32[8,3,16,1,128]{4,2,1,0,3:T(8,128)S(1)} %get-tuple-element.55), channel_id=1, source_target_pairs={{0,12},{4,16},{8,20},{12,24},{16,28},{20,0},{24,4},{28,8},{1,13},{... | collective-permute-start | bytes 589832 | tf_op jit(solution)/shard_map/ppermute | solution.py:168
  161.8 15.1 %collective-permute-start.7 = (f32[8,3,16,1,128]{4,2,1,0,3:T(8,128)S(1)}, f32[8,3,16,1,128]{4,2,1,0,3:T(8,128)S(1)}, u32[]{:S(2)}, u32[]{:S(2)}) collective-permute-start(f32[8,3,16,1,128]{4,2,1,0,3:T(8,128)S(1)} %get-tuple-element.54), channel_id=1, source_target_pairs={{0,8},{4,12},{8,16},{12,20},{16,24},{20,28},{24,0},{28,4},{1,9},{5... | collective-permute-start | bytes 589832 | tf_op jit(solution)/shard_map/ppermute | solution.py:168
  165.9 11.1 %collective-permute-start.8 = (f32[8,3,16,1,128]{4,2,1,0,3:T(8,128)S(1)}, f32[8,3,16,1,128]{4,2,1,0,3:T(8,128)S(1)}, u32[]{:S(2)}, u32[]{:S(2)}) collective-permute-start(f32[8,3,16,1,128]{4,2,1,0,3:T(8,128)S(1)} %get-tuple-element.53), channel_id=1, source_target_pairs={{0,4},{4,8},{8,12},{12,16},{16,20},{20,24},{24,28},{28,0},{1,5},{5... | collective-permute-start | bytes 589832 | tf_op jit(solution)/shard_map/ppermute | solution.py:168
  177.6 5.0 %copy-start.2 = (pred[256]{0:T(512)(128)(4,1)S(1)}, pred[256]{0:T(512)(128)(4,1)}, u32[]{:S(2)}) copy-start(pred[256]{0:T(512)(128)(4,1)} %compare_and_fusion) | copy-start | bytes 772
  177.6 5.0 %copy-start.3 = (f32[1,1,256]{2,1,0:T(1,128)S(1)}, f32[1,1,256]{2,1,0:T(1,128)}, u32[]{:S(2)}) copy-start(f32[1,1,256]{2,1,0:T(1,128)} %param.11) | copy-start | bytes 3076
  182.7 2.5 %collective-permute-start.10 = (f32[1,1,68,256]{3,2,1,0:T(8,128)S(1)}, f32[1,1,68,256]{3,2,1,0:T(8,128)S(1)}, u32[]{:S(2)}, u32[]{:S(2)}) collective-permute-start(f32[1,1,68,256]{3,2,1,0:T(8,128)S(1)} %bitcast.261), channel_id=1, source_target_pairs={{4,0},{8,4},{12,8},{16,12},{20,16},{24,20},{28,24},{0,28},{5,1},{9... | collective-permute-start | bytes 208904 | tf_op jit(solution)/shard_map/ppermute | solution.py:25
  182.7 4.7 %collective-permute-start.9 = (f32[1,1,68,256]{3,2,1,0:T(8,128)S(1)}, f32[1,1,68,256]{3,2,1,0:T(8,128)S(1)}, u32[]{:S(2)}, u32[]{:S(2)}) collective-permute-start(f32[1,1,68,256]{3,2,1,0:T(8,128)S(1)} %bitcast.262), channel_id=1, source_target_pairs={{0,4},{4,8},{8,12},{12,16},{16,20},{20,24},{24,28},{28,0},{1,5},{5... | collective-permute-start | bytes 208904 | tf_op jit(solution)/shard_map/ppermute | solution.py:22
  187.5 9.4 %collective-permute-start.11 = (f32[1,3,68,256]{3,2,1,0:T(8,128)S(1)}, f32[1,3,68,256]{3,2,1,0:T(8,128)S(1)}, u32[]{:S(2)}, u32[]{:S(2)}) collective-permute-start(f32[1,3,68,256]{3,2,1,0:T(8,128)S(1)} %pad_maximum_fusion.3), channel_id=1, source_target_pairs={{0,1},{1,2},{2,3},{3,0},{4,5},{5,6},{6,7},{7,4},{8,9},{9,10},{10,1... | collective-permute-start | bytes 626696 | tf_op jit(solution)/shard_map/ppermute | solution.py:22
  189.4 9.5 %collective-permute-start.12 = (f32[1,3,68,256]{3,2,1,0:T(8,128)S(1)}, f32[1,3,68,256]{3,2,1,0:T(8,128)S(1)}, u32[]{:S(2)}, u32[]{:S(2)}) collective-permute-start(f32[1,3,68,256]{3,2,1,0:T(8,128)S(1)} %pad_maximum_fusion.3), channel_id=1, source_target_pairs={{1,0},{2,1},{3,2},{0,3},{5,4},{6,5},{7,6},{4,7},{9,8},{10,9},{11,1... | collective-permute-start | bytes 626696 | tf_op jit(solution)/shard_map/ppermute | solution.py:25
